TPU v7x, 256 devices: a whole 4x4x8 slice. The times are simulated.
256 devices in a mesh: dp: 8 (over y, core), expert: 8 (over z), tile: 4 (over x).
Axes of the slice: x: 4, y: 4, z: 8, core: 2. Of those that a mesh axis runs over, the one named last changes fastest.
Arguments:
- tokens: bfloat16 [4096, 4096], P(('dp', 'expert'), 'tile'), may hold values from -6 to 6
- hidden: bfloat16 [4096, 2, 7168], P(('dp', 'expert'), None, 'tile'), may hold values from -6 to 6
- routes: int32 [4096, 2], P(('dp', 'expert')), may hold values from 0 to 7, all different within a row; in each aligned block of 64 rows (0 to 63, 64 to 127, ...) at most 24 rows name the same one
- lengths: int32 [64], P(('dp', 'expert')), may hold values from 1 to 64, as said below
Outputs:
- hessian_in: float32 [8, 4096, 4096], P('expert', 'tile', 'dp')
- hessian_down: float32 [8, 7168, 7168], P('expert', 'tile', 'dp')
Inputs may be any that keep to these rules, and one draw needn't show every extreme that they name: `routes`: in each aligned block of 64 rows (the rows of one group) no expert is named by more than 24 rows, a bound that some block reaches. The live rows of group g are its first lengths[g] rows; the last group is full.
All inputs are finite; a program needn't handle non-finite values.
Results may differ from a plain program's by a relative error of at most 0.0003.
Values may be sent and summed in bfloat16 or wider, within the bound.
A program may use at most 64 MiB of HBM per device.

v0:
```python
import jax
import jax.numpy as jnp
from jax import lax
from jax.sharding import PartitionSpec as P


def sent_together(arrays, axis, split_dim, concat_dim, along):
    widths = [a.shape[along] for a in arrays]
    both = jnp.concatenate(arrays, axis=along)
    out = lax.all_to_all(both, axis, split_axis=split_dim, concat_axis=concat_dim, tiled=True)
    return tuple(jnp.split(out, [sum(widths[:k]) for k in range(1, len(widths))], axis=along))


def from_everyone(value, axis):
    copies = jnp.broadcast_to(value, (lax.axis_size(axis), *value.shape))
    return lax.all_to_all(copies, axis, split_axis=0, concat_axis=0, tiled=True)


def of_everyone(value, axis):
    everything = from_everyone(value, axis)
    return jnp.sum(everything, axis=0)


def side_by_side(arrays, axis, dim, along):
    ends, at = ([], 0)
    for a in arrays[:-1]:
        at += a.shape[along]
        ends.append(at)
    both = jnp.concatenate(arrays, axis=along)
    return tuple(jnp.split(lax.all_gather(both, axis, axis=dim, tiled=True), ends, axis=along))


def contract(left, right):
    return lax.dot_general(
        left, right, (((0,), (0,)), ((), ())), preferred_element_type=jnp.float32
    )


def dispatch_tables(routes, live_count, experts, share_size, senders):
    token_count = routes.shape[0]
    top_count = routes.shape[1]
    flat_routes = routes.reshape(token_count * top_count)
    pair_index = jnp.arange(token_count * top_count, dtype=jnp.int32)
    pair_live = pair_index // top_count < live_count
    expert_ids = jnp.arange(experts, dtype=jnp.int32)
    onehot = ((flat_routes[:, None] == expert_ids[None, :]) & pair_live[:, None]).astype(
        jnp.float32
    )
    before = jnp.cumsum(onehot, axis=0) - onehot
    position = jnp.sum(before * onehot, axis=1).astype(jnp.int32)
    target = (
        position // share_size * (experts * share_size)
        + flat_routes * share_size
        + position % share_size
    )
    slot_total = senders * experts * share_size
    placed = (target[None, :] == jnp.arange(slot_total, dtype=jnp.int32)[:, None]) & pair_live[
        None, :
    ]
    return (placed.astype(jnp.float32), jnp.sum(onehot, axis=0))


def on_device(tokens, hidden, routes, lengths):
    experts = lax.axis_size("expert")
    senders = lax.axis_size("dp")
    token_count = tokens.shape[0]
    top_count = routes.shape[1]
    share_size = (5 * token_count + 2 * experts * senders - 1) // (2 * experts * senders)
    placed, local_counts = dispatch_tables(routes, lengths[0], experts, share_size, senders)
    slot_total = placed.shape[0]
    by_token = jnp.sum(placed.reshape(slot_total, token_count, top_count), axis=2).astype(
        jnp.bfloat16
    )
    send_tokens = jnp.dot(by_token, tokens, preferred_element_type=jnp.float32).astype(jnp.bfloat16)
    flat_hidden = hidden.reshape(token_count * top_count, hidden.shape[2])
    send_hidden = jnp.dot(
        placed.astype(jnp.bfloat16), flat_hidden, preferred_element_type=jnp.float32
    ).astype(jnp.bfloat16)
    slot_tokens, slot_hidden = sent_together((send_tokens, send_hidden), ("dp", "expert"), 0, 0, 1)
    global_counts = of_everyone(local_counts, ("dp", "expert"))
    own_expert = lax.axis_index("expert")
    own_count = jnp.sum(
        jnp.where(jnp.arange(experts, dtype=jnp.int32) == own_expert, global_counts, 0.0)
    )
    factor = 2.0 / jnp.maximum(own_count, 1.0)
    full_tokens, full_hidden = (
        lax.all_gather(slot_tokens, "tile", axis=1, tiled=True),
        lax.all_gather(slot_hidden, "tile", axis=1, tiled=True),
    )
    column_tokens, column_hidden = (
        lax.all_to_all(full_tokens, "dp", split_axis=1, concat_axis=0, tiled=True),
        lax.all_to_all(full_hidden, "dp", split_axis=1, concat_axis=0, tiled=True),
    )
    pieces = side_by_side((slot_tokens, slot_hidden), "dp", 0, 1)
    gram_tokens = contract(pieces[0], column_tokens)
    gram_hidden = contract(pieces[1], column_hidden)
    return ((gram_tokens * factor)[None], (gram_hidden * factor)[None])


def solution(mesh):
    placed = (
        P(("dp", "expert"), "tile"),
        P(("dp", "expert"), None, "tile"),
        P(("dp", "expert"), None),
        P(("dp", "expert")),
    )
    return jax.shard_map(
        on_device,
        mesh=mesh,
        in_specs=placed,
        out_specs=(P("expert", "tile", "dp"), P("expert", "tile", "dp")),
        check_vma=False,
    )
```

profile of v0, /device:TPU:1, one launch (start us, length us, event | category | flops | bytes accessed | tf_op | source)
XLA Modules:
  0.0 226.2 jit_solution(10405702550066354825)
XLA Ops:
  7.2 0.0 copy-start
  7.2 0.0 all-gather.8.cloned.1.call-start
  7.9 0.8 copy.33
  8.7 0.1 eq.43
  8.8 0.1 fusion.11
  8.9 0.2 reduce_window_sum.11
  9.1 0.2 fusion.12
  9.3 0.1 rem.32
  9.5 0.1 copy.34
  9.5 0.1 div.25
  9.7 0.1 copy.36
  9.8 0.2 ne.82
  9.9 0.1 copy.35
  10.1 1.2 reshape.98
  11.2 0.7 fusion.18
  11.9 0.1 convert_reduce_fusion
  12.1 0.0 copy-done
  12.1 0.3 convolution_convert_fusion.1
  12.3 0.3 convolution_convert_fusion
  12.7 0.1 pad_maximum_fusion
  12.8 0.5 all_to_all.40
  13.3 49.6 %all_to_all.56 = bf16[64,3,2816]{2,1,0:T(4,128)(2,1)S(1)} all-to-all(bf16[64,3,2816]{2,1,0:T(4,128)(2,1)S(1)} %all_to_all.40), channel_id=1, replica_groups=mesh['dp'=8,'expert'=8,'tile'=4] {'dp','expert'}, dimensions={0} | all-to-all | bytes 2162688 | tf_op jit(solution)/shard_map/all_to_all | solution.py:10
  62.8 0.9 all_to_all.42
  63.8 0.0 copy-start.1
  63.8 1.0 split.19
  64.8 0.0 all-gather.8.cloned.1.call-update
  64.8 0.0 all-gather.6.cloned.1.call-start
  64.8 0.8 split.17
  65.7 0.0 all-gather.6.cloned.1.call-update
  65.7 0.0 all-gather.4.cloned.1.call-start
  65.7 0.0 copy-done.1
  65.7 0.7 all-gather.4.cloned.1.call-update
  66.4 0.6 broadcast_in_dim.18
  67.0 6.7 %all-to-all-start.2 = ((f32[64,1,8]{2,1,0:T(1,128)}), f32[64,1,8]{2,1,0:T(1,128)S(1)}, u32[]{:S(2)}, u32[]{:S(2)}) async-start(f32[64,1,8]{2,1,0:T(1,128)} %broadcast_in_dim.18), calls=%async_computation.2 | async-start | bytes 65536 | tf_op jit(solution)/shard_map/all_to_all | solution.py:16
  73.8 27.1 %all-gather.8.cloned.1.call-done = bf16[192,7168]{1,0:T(8,128)(2,1)} async-done(((bf16[192,1792]{1,0:T(8,128)(2,1)}), bf16[192,7168]{1,0:T(8,128)(2,1)}) %all-gather.8.cloned.1.call-update) | async-done | bytes 2752528 | tf_op jit(solution)/shard_map/all_gather | solution.py:88
  100.9 3.7 %copy.49 = bf16[24,8,8,896]{3,2,0,1:T(8,128)(2,1)} copy(bf16[24,8,8,896]{3,2,1,0:T(8,128)(2,1)} %bitcast.27) | data formatting | bytes 5505024 | tf_op jit(solution)/shard_map/all_to_all | solution.py:92
  104.6 0.0 all-to-all-done.2
  104.6 5.1 %all-to-all-start.3 = ((bf16[192,8,896]{2,0,1:T(8,128)(2,1)}), bf16[192,8,896]{2,0,1:T(8,128)(2,1)S(1)}, u32[]{:S(2)}, u32[]{:S(2)}) async-start(bf16[192,8,896]{2,0,1:T(8,128)(2,1)} %bitcast.22), calls=%async_computation.3 | async-start | bytes 5505024 | tf_op jit(solution)/shard_map/all_to_all | solution.py:92
  109.7 22.2 %all-gather.6.cloned.1.call-done = bf16[192,4096]{1,0:T(8,128)(2,1)} async-done(((bf16[192,1024]{1,0:T(8,128)(2,1)}), bf16[192,4096]{1,0:T(8,128)(2,1)}) %all-gather.6.cloned.1.call-update) | async-done | bytes 1572880 | tf_op jit(solution)/shard_map/all_gather | solution.py:87
  131.9 2.7 %copy.50 = bf16[24,8,8,512]{3,2,0,1:T(8,128)(2,1)} copy(bf16[24,8,8,512]{3,2,1,0:T(8,128)(2,1)} %bitcast.28) | data formatting | bytes 3145728 | tf_op jit(solution)/shard_map/all_to_all | solution.py:91
  134.6 8.4 %all-to-all-done.3 = bf16[192,8,896]{2,0,1:T(8,128)(2,1)S(1)} async-done(((bf16[192,8,896]{2,0,1:T(8,128)(2,1)}), bf16[192,8,896]{2,0,1:T(8,128)(2,1)S(1)}, u32[]{:S(2)}, u32[]{:S(2)}) %all-to-all-start.3) | async-done | bytes 2752544 | tf_op jit(solution)/shard_map/all_to_all | solution.py:92
  142.9 5.2 %all-to-all-start.1 = ((bf16[192,8,512]{2,0,1:T(8,128)(2,1)}), bf16[192,8,512]{2,0,1:T(8,128)(2,1)}, u32[]{:S(2)}, u32[]{:S(2)}) async-start(bf16[192,8,512]{2,0,1:T(8,128)(2,1)} %bitcast.23), calls=%async_computation.1 | async-start | bytes 3145728 | tf_op jit(solution)/shard_map/all_to_all | solution.py:91
  148.1 0.1 reduce_sum.48
  148.2 0.6 fusion.22
  149.5 55.0 %all-gather.4.cloned.1.call-done = bf16[1536,2816]{1,0:T(8,128)(2,1)} async-done(((bf16[192,2816]{1,0:T(8,128)(2,1)}), bf16[1536,2816]{1,0:T(8,128)(2,1)}) %all-gather.4.cloned.1.call-update) | async-done | bytes 8650768 | tf_op jit(solution)/shard_map/all_gather | solution.py:30
  204.5 9.6 %multiply_bitcast_fusion = f32[1,1792,896]{2,1,0:T(8,128)} fusion(bf16[1536,896]{1,0:T(8,128)(2,1)S(1)} %bitcast.26, bf16[1536,2816]{1,0:T(8,128)(2,1)} %all-gather.4.cloned.1.call-done, f32[]{:T(128)S(6)} %div.27), kind=kOutput, calls=%fused_computation | convolution fusion | flops 4934107136 | bytes 14680068 | tf_op jit(solution)/shard_map/dot_general | solution.py:34
  214.2 0.0 all-to-all-done.1
  214.2 5.5 %multiply_bitcast_fusion.1 = f32[1,1024,512]{2,1,0:T(8,128)} fusion(bf16[1536,512]{1,0:T(8,128)(2,1)} %bitcast.2, bf16[1536,2816]{1,0:T(8,128)(2,1)} %all-gather.4.cloned.1.call-done, f32[]{:T(128)S(6)} %div.27), kind=kOutput, calls=%fused_computation.7 | convolution fusion | flops 1611137024 | bytes 6815748 | tf_op jit(solution)/shard_map/dot_general | solution.py:34
  (4 shorter events, 0.1 us)
Async XLA Ops:
  7.2 4.9 %copy-start = (bf16[64,1024]{1,0:T(8,128)(2,1)S(1)}, bf16[64,1024]{1,0:T(8,128)(2,1)}, u32[]{:S(2)}) copy-start(bf16[64,1024]{1,0:T(8,128)(2,1)} %param.4) | copy-start | bytes 393220
  7.2 93.7 %all-gather.8.cloned.1.call-start = ((), (), s32[]{:S(2)}) async-start(), calls=%async_computation.6 | async-start | bytes 3440640 | tf_op jit(solution)/shard_map/all_gather | solution.py:88
  63.8 2.0 copy-start.1
  64.8 67.1 %all-gather.6.cloned.1.call-start = ((), (), s32[]{:S(2)}) async-start(), calls=%async_computation.5 | async-start | bytes 1966080 | tf_op jit(solution)/shard_map/all_gather | solution.py:87
  65.7 138.8 %all-gather.4.cloned.1.call-start = ((), (), s32[]{:S(2)}) async-start(), calls=%async_computation.4 | async-start | bytes 9732096 | tf_op jit(solution)/shard_map/all_gather | solution.py:30
  67.0 37.5 %all-to-all-start.2 = ((f32[64,1,8]{2,1,0:T(1,128)}), f32[64,1,8]{2,1,0:T(1,128)S(1)}, u32[]{:S(2)}, u32[]{:S(2)}) async-start(f32[64,1,8]{2,1,0:T(1,128)} %broadcast_in_dim.18), calls=%async_computation.2 | async-start | bytes 65536 | tf_op jit(solution)/shard_map/all_to_all | solution.py:16
  104.6 38.4 %all-to-all-start.3 = ((bf16[192,8,896]{2,0,1:T(8,128)(2,1)}), bf16[192,8,896]{2,0,1:T(8,128)(2,1)S(1)}, u32[]{:S(2)}, u32[]{:S(2)}) async-start(bf16[192,8,896]{2,0,1:T(8,128)(2,1)} %bitcast.22), calls=%async_computation.3 | async-start | bytes 5505024 | tf_op jit(solution)/shard_map/all_to_all | solution.py:92
  142.9 71.2 %all-to-all-start.1 = ((bf16[192,8,512]{2,0,1:T(8,128)(2,1)}), bf16[192,8,512]{2,0,1:T(8,128)(2,1)}, u32[]{:S(2)}, u32[]{:S(2)}) async-start(bf16[192,8,512]{2,0,1:T(8,128)(2,1)} %bitcast.23), calls=%async_computation.1 | async-start | bytes 3145728 | tf_op jit(solution)/shard_map/all_to_all | solution.py:91
Sparse Core Ops, SparseCore 0:
  64.9 35.9 all-gather.7
  102.7 29.1 all-gather.5
  133.7 70.7 all-gather.3
where the time goes:
time: 227 us; the launch traced here: 226 us
  waiting for transfers between devices  113 us (50%)
  blocking collectives  49.6 us (22%)
  starting transfers between devices  17.1 us (8%)
  matrix products  15.8 us (7%)
  between operations  15.3 us (7%)
  local copies, waits for them, and re-layouts  13 us (6%)
    all_gather x1, waiting for transfers between devices, side_by_side(): lax.all_gather(both, axis, axis=dim, tiled=True)  55 us
    all_to_all x1, blocking collectives, sent_together(): lax.all_to_all(both, axis, split_axis=split_dim, concat_axis=concat_dim,...  49.6 us
    all_gather x1, waiting for transfers between devices, on_device(): lax.all_gather(slot_hidden, 'tile', axis=1, tiled=True)  27.1 us
    all_gather x1, waiting for transfers between devices, on_device(): lax.all_gather(slot_tokens, 'tile', axis=1, tiled=True)  22.2 us
    dot_general x2, matrix products, contract(): lax.dot_general(left, right, (((0,), (0,)), ((), ())), preferred_element_...  15.2 us
    all_to_all x1, waiting for transfers between devices, on_device(): lax.all_to_all(full_hidden, 'dp', split_axis=1, concat_axis=0, tiled=True)  8.35 us
    all_to_all x1, starting transfers between devices, from_everyone(): return lax.all_to_all(copies, axis, split_axis=0, concat_axis=0, tiled=True)  6.72 us
    all_to_all x1, starting transfers between devices, on_device(): lax.all_to_all(full_tokens, 'dp', split_axis=1, concat_axis=0, tiled=True)  5.17 us
  transfers between devices with their start and end apart: 6, of which 4 were waited for; matrix products, arithmetic and copies ran while one was open for 8% of the time, Pallas kernels for 0%

commit v1 on v0

--- a/solution.py
+++ b/solution.py
@@ -2,6 +2,12 @@
 import jax.numpy as jnp
 from jax import lax
 from jax.sharding import PartitionSpec as P
+
+
+def stack_and_merge(x, axis, dim):
+    shards = lax.all_gather(x, axis, axis=0, tiled=False)
+    whole = jnp.concatenate(shards, axis=dim)
+    return whole
 
 
 def sent_together(arrays, axis, split_dim, concat_dim, along):
@@ -84,7 +90,7 @@
     )
     factor = 2.0 / jnp.maximum(own_count, 1.0)
     full_tokens, full_hidden = (
-        lax.all_gather(slot_tokens, "tile", axis=1, tiled=True),
+        stack_and_merge(slot_tokens, "tile", 1),
         lax.all_gather(slot_hidden, "tile", axis=1, tiled=True),
     )
     column_tokens, column_hidden = (

time: 227 us -> 227 us (level)
    all_gather x0 -> x1, local copies, waits for them, and re-layouts: none -> 2.62 us  [stack_and_merge(): shards = lax.all_gather(x, axis, axis=0, tiled=False)]
  transfers between devices with their start and end apart: 6 -> 6, of which waited for: 4 -> 4; matrix products, arithmetic and copies ran while one was open for 8% -> 9% of each run, Pallas kernels for 0% -> 0%
where the time goes in v1:
time: 227 us
  waiting for transfers between devices  112 us (49%)
  blocking collectives  49.6 us (22%)
  starting transfers between devices  16.5 us (7%)
  matrix products  16.1 us (7%)
  between operations  15.3 us (7%)
  local copies, waits for them, and re-layouts  15 us (7%)
    all_gather x1, waiting for transfers between devices, side_by_side(): lax.all_gather(both, axis, axis=dim, tiled=True)  55.6 us
    all_to_all x1, blocking collectives, sent_together(): lax.all_to_all(both, axis, split_axis=split_dim, concat_axis=concat_dim,...  49.6 us
    all_gather x1, waiting for transfers between devices, on_device(): lax.all_gather(slot_hidden, 'tile', axis=1, tiled=True)  27.1 us
    all_gather x1, waiting for transfers between devices, stack_and_merge(): shards = lax.all_gather(x, axis, axis=0, tiled=False)  22.1 us
    dot_general x2, matrix products, contract(): lax.dot_general(left, right, (((0,), (0,)), ((), ())), preferred_element_...  15.5 us
    all_to_all x1, starting transfers between devices, from_everyone(): return lax.all_to_all(copies, axis, split_axis=0, concat_axis=0, tiled=True)  6.72 us
    all_to_all x1, waiting for transfers between devices, on_device(): lax.all_to_all(full_hidden, 'dp', split_axis=1, concat_axis=0, tiled=True)  6.5 us
    all_to_all x1, starting transfers between devices, on_device(): lax.all_to_all(full_hidden, 'dp', split_axis=1, concat_axis=0, tiled=True)  5.15 us
  transfers between devices with their start and end apart: 6, of which 4 were waited for; matrix products, arithmetic and copies ran while one was open for 9% of the time, Pallas kernels for 0%

profile of v1, /device:TPU:1, one launch (start us, length us, event | category | flops | bytes accessed | tf_op | source)
XLA Modules:
  0.0 226.5 jit_solution(17701793265951929657)
XLA Ops:
  7.2 0.0 copy-start
  7.2 0.0 all-gather.7.cloned.1.call-start
  7.9 0.8 copy.43
  8.7 0.1 eq.43
  8.8 0.1 fusion.11
  8.9 0.2 reduce_window_sum.11
  9.1 0.2 fusion.12
  9.3 0.1 rem.32
  9.5 0.1 copy.44
  9.5 0.1 div.25
  9.7 0.1 copy.46
  9.8 0.2 ne.82
  9.9 0.1 copy.45
  10.1 1.2 reshape.103
  11.2 0.7 fusion.18
  11.9 0.1 convert_reduce_fusion
  12.1 0.0 copy-done
  12.1 0.3 convolution_convert_fusion.1
  12.3 0.3 convolution_convert_fusion
  12.7 0.1 pad_maximum_fusion
  12.8 0.5 all_to_all.40
  13.3 49.6 %all_to_all.56 = bf16[64,3,2816]{2,1,0:T(4,128)(2,1)S(1)} all-to-all(bf16[64,3,2816]{2,1,0:T(4,128)(2,1)S(1)} %all_to_all.40), channel_id=1, replica_groups=mesh['dp'=8,'expert'=8,'tile'=4] {'dp','expert'}, dimensions={0} | all-to-all | bytes 2162688 | tf_op jit(solution)/shard_map/all_to_all | solution.py:16
  62.8 0.9 all_to_all.42
  63.8 1.0 split.19
  64.8 0.0 all-gather.7.cloned.1.call-update
  64.8 0.0 all-gather.9.cloned.1.call-start
  64.8 0.8 split.17
  65.7 0.0 all-gather.9.cloned.1.call-update
  65.7 0.0 all-gather.5.cloned.1.call-start
  65.7 0.7 all-gather.5.cloned.1.call-update
  66.4 0.6 broadcast_in_dim.18
  67.0 6.7 %all-to-all-start.2 = ((f32[64,1,8]{2,1,0:T(1,128)}), f32[64,1,8]{2,1,0:T(1,128)S(1)}, u32[]{:S(2)}, u32[]{:S(2)}) async-start(f32[64,1,8]{2,1,0:T(1,128)} %broadcast_in_dim.18), calls=%async_computation.2 | async-start | bytes 65536 | tf_op jit(solution)/shard_map/all_to_all | solution.py:22
  73.8 27.1 %all-gather.7.cloned.1.call-done = bf16[192,7168]{1,0:T(8,128)(2,1)} async-done(((bf16[192,1792]{1,0:T(8,128)(2,1)}), bf16[192,7168]{1,0:T(8,128)(2,1)}) %all-gather.7.cloned.1.call-update) | async-done | bytes 2752528 | tf_op jit(solution)/shard_map/all_gather | solution.py:94
  100.9 3.7 %copy.59 = bf16[24,8,8,896]{3,2,0,1:T(8,128)(2,1)} copy(bf16[24,8,8,896]{3,2,1,0:T(8,128)(2,1)} %bitcast.27) | data formatting | bytes 5505024 | tf_op jit(solution)/shard_map/all_to_all | solution.py:98
  104.6 0.0 all-to-all-done.2
  104.6 5.1 %all-to-all-start.3 = ((bf16[192,8,896]{2,0,1:T(8,128)(2,1)}), bf16[192,8,896]{2,0,1:T(8,128)(2,1)}, u32[]{:S(2)}, u32[]{:S(2)}) async-start(bf16[192,8,896]{2,0,1:T(8,128)(2,1)} %bitcast.22), calls=%async_computation.3 | async-start | bytes 5505024 | tf_op jit(solution)/shard_map/all_to_all | solution.py:98
  109.7 22.1 %all-gather.9.cloned.1.call-done = bf16[768,1024]{1,0:T(8,128)(2,1)} async-done(((bf16[192,1024]{1,0:T(8,128)(2,1)}), bf16[768,1024]{1,0:T(8,128)(2,1)}) %all-gather.9.cloned.1.call-update) | async-done | bytes 1572880 | tf_op jit(solution)/shard_map/all_gather | solution.py:8
  131.9 2.6 %copy.60 = bf16[4,192,1024]{2,0,1:T(4,128)(2,1)S(1)} copy(bf16[4,192,1024]{2,1,0:T(8,128)(2,1)} %bitcast.28) | data formatting | bytes 3145728 | tf_op jit(solution)/shard_map/all_gather | solution.py:8
  134.5 0.4 all_to_all.43
  134.9 1.6 copy.52
  136.6 6.5 %all-to-all-done.3 = bf16[192,8,896]{2,0,1:T(8,128)(2,1)} async-done(((bf16[192,8,896]{2,0,1:T(8,128)(2,1)}), bf16[192,8,896]{2,0,1:T(8,128)(2,1)}, u32[]{:S(2)}, u32[]{:S(2)}) %all-to-all-start.3) | async-done | bytes 2752544 | tf_op jit(solution)/shard_map/all_to_all | solution.py:98
  143.1 4.5 %all-to-all-start.1 = ((bf16[192,8,512]{2,0,1:T(8,128)(2,1)}), bf16[192,8,512]{2,0,1:T(8,128)(2,1)S(1)}, u32[]{:S(2)}, u32[]{:S(2)}) async-start(bf16[192,8,512]{2,0,1:T(8,128)(2,1)} %copy.52), calls=%async_computation.1 | async-start | bytes 3145728 | tf_op jit(solution)/shard_map/all_to_all | solution.py:97
  147.6 0.1 reduce_sum.48
  147.7 0.6 fusion.22
  149.0 55.6 %all-gather.5.cloned.1.call-done = bf16[1536,2816]{1,0:T(8,128)(2,1)} async-done(((bf16[192,2816]{1,0:T(8,128)(2,1)}), bf16[1536,2816]{1,0:T(8,128)(2,1)}) %all-gather.5.cloned.1.call-update) | async-done | bytes 8650768 | tf_op jit(solution)/shard_map/all_gather | solution.py:36
  204.5 10.4 %multiply_bitcast_fusion = f32[1,1792,896]{2,1,0:T(8,128)} fusion(bf16[1536,896]{1,0:T(8,128)(2,1)} %bitcast.7, bf16[1536,2816]{1,0:T(8,128)(2,1)} %all-gather.5.cloned.1.call-done, f32[]{:T(128)S(6)} %div.27), kind=kOutput, calls=%fused_computation | convolution fusion | flops 4934107136 | bytes 14680068 | tf_op jit(solution)/shard_map/dot_general | solution.py:40
  215.0 0.0 all-to-all-done.1
  215.0 5.1 %multiply_bitcast_fusion.1 = f32[1,1024,512]{2,1,0:T(8,128)} fusion(bf16[1536,512]{1,0:T(8,128)(2,1)S(1)} %bitcast.29, bf16[1536,2816]{1,0:T(8,128)(2,1)} %all-gather.5.cloned.1.call-done, f32[]{:T(128)S(6)} %div.27), kind=kOutput, calls=%fused_computation.7 | convolution fusion | flops 1611137024 | bytes 6815748 | tf_op jit(solution)/shard_map/dot_general | solution.py:40
  (6 shorter events, 0.1 us)
Async XLA Ops:
  7.2 4.9 %copy-start = (bf16[64,1024]{1,0:T(8,128)(2,1)S(1)}, bf16[64,1024]{1,0:T(8,128)(2,1)}, u32[]{:S(2)}) copy-start(bf16[64,1024]{1,0:T(8,128)(2,1)} %param.4) | copy-start | bytes 393220
  7.2 93.7 %all-gather.7.cloned.1.call-start = ((), (), s32[]{:S(2)}) async-start(), calls=%async_computation.5 | async-start | bytes 3440640 | tf_op jit(solution)/shard_map/all_gather | solution.py:94
  63.8 2.0 copy-start.1
  64.8 67.1 %all-gather.9.cloned.1.call-start = ((), (), s32[]{:S(2)}) async-start(), calls=%async_computation.6 | async-start | bytes 1966080 | tf_op jit(solution)/shard_map/all_gather | solution.py:8
  65.7 138.8 %all-gather.5.cloned.1.call-start = ((), (), s32[]{:S(2)}) async-start(), calls=%async_computation.4 | async-start | bytes 9732096 | tf_op jit(solution)/shard_map/all_gather | solution.py:36
  67.0 37.5 %all-to-all-start.2 = ((f32[64,1,8]{2,1,0:T(1,128)}), f32[64,1,8]{2,1,0:T(1,128)S(1)}, u32[]{:S(2)}, u32[]{:S(2)}) async-start(f32[64,1,8]{2,1,0:T(1,128)} %broadcast_in_dim.18), calls=%async_computation.2 | async-start | bytes 65536 | tf_op jit(solution)/shard_map/all_to_all | solution.py:22
  104.6 38.5 %all-to-all-start.3 = ((bf16[192,8,896]{2,0,1:T(8,128)(2,1)}), bf16[192,8,896]{2,0,1:T(8,128)(2,1)}, u32[]{:S(2)}, u32[]{:S(2)}) async-start(bf16[192,8,896]{2,0,1:T(8,128)(2,1)} %bitcast.22), calls=%async_computation.3 | async-start | bytes 5505024 | tf_op jit(solution)/shard_map/all_to_all | solution.py:98
  143.1 71.9 %all-to-all-start.1 = ((bf16[192,8,512]{2,0,1:T(8,128)(2,1)}), bf16[192,8,512]{2,0,1:T(8,128)(2,1)S(1)}, u32[]{:S(2)}, u32[]{:S(2)}) async-start(bf16[192,8,512]{2,0,1:T(8,128)(2,1)} %copy.52), calls=%async_computation.1 | async-start | bytes 3145728 | tf_op jit(solution)/shard_map/all_to_all | solution.py:97
Sparse Core Ops, SparseCore 0:
  64.9 35.9 all-gather.6
  102.7 29.1 all-gather.8
  133.7 70.7 all-gather.4
